TPU v7x, 32 devices: a whole 2x2x4 slice. The times are simulated.
32 devices in a mesh: cuts: 4 (over z), dev: 8 (over y, x, core).
Axes of the slice: x: 2, y: 2, z: 4, core: 2. Of those that a mesh axis runs over, the one named last changes fastest.
Arguments:
- inputs: bfloat16 [16384, 3072], P(('cuts', 'dev')), may hold values from -6 to 6
- cotangent: bfloat16 [16384, 512], P(('cuts', 'dev')), may hold values from -0.29882812 to 0.29882812
- errors: bfloat16 [32, 3072, 512], P(('cuts', 'dev')), may hold values from -6 to 6
- previous_q: float32 [512, 64], replicated, may hold values from -0.25 to 0.25
Outputs:
- new_errors: bfloat16 [32, 3072, 512], P(('cuts', 'dev'))
- p_hat: float32 [3072, 64], replicated
- q_mean: float32 [512, 64], replicated
All inputs are finite; a program needn't handle non-finite values.
Results may differ from a plain program's by a relative error of at most 0.001.
Values sent between devices are 32-bit elements; how exact they have to be, the bound alone decides.
No kernel may reach another device: no remote copies, remote signals or barrier semaphores. Data moves between devices by JAX's collectives and lax.ppermute only.
A program may use at most 64 MiB of HBM per device.

v0:
```python
import jax
import jax.numpy as jnp
from jax import lax
from jax.sharding import PartitionSpec as P

HI = lax.Precision.HIGHEST


def solve_factor(gram, p_rows):
    lower = jnp.linalg.cholesky(gram)
    return lax.linalg.triangular_solve(lower, p_rows, left_side=False, lower=True, transpose_a=True)


def contract_rows(left, right):
    return lax.dot_general(
        left, right, (((0,), (0,)), ((), ())), precision=HI, preferred_element_type=jnp.float32
    )


def body(inputs, cotangent, errors, previous_q):
    grad = lax.dot_general(
        inputs, cotangent, (((0,), (0,)), ((), ())), preferred_element_type=jnp.float32
    )
    merged = grad + errors[0].astype(jnp.float32)
    devices = lax.axis_size("cuts") * lax.axis_size("dev")
    p_share = lax.psum_scatter(
        jnp.dot(merged, previous_q, precision=HI), "dev", scatter_dimension=0, tiled=True
    )
    p_share = lax.psum(p_share, "cuts")
    gram = lax.psum(contract_rows(p_share, p_share), "dev")
    hat_share = solve_factor(gram, p_share)
    p_hat = lax.all_gather(hat_share, "dev", axis=0, tiled=True)
    q_share = lax.psum_scatter(contract_rows(merged, p_hat), "dev", scatter_dimension=0, tiled=True)
    q_share = lax.psum(q_share, "cuts")
    q_sum = lax.all_gather(q_share, "dev", axis=0, tiled=True)
    q_mean = q_sum / devices
    approx = jnp.dot(p_hat, q_mean.T, precision=HI)
    new_errors = (merged - approx).astype(jnp.bfloat16)[None]
    return (new_errors, p_hat, q_mean)


def solution(mesh):
    in_specs = (
        P(("cuts", "dev"), None),
        P(("cuts", "dev"), None),
        P(("cuts", "dev"), None, None),
        P(),
    )
    out_specs = (P(("cuts", "dev"), None, None), P(), P())
    return jax.shard_map(body, mesh=mesh, in_specs=in_specs, out_specs=out_specs, check_vma=False)
```

profile of v0, /device:TPU:0, one launch (start us, length us, event | category | flops | bytes accessed | tf_op | source)
XLA Modules:
  0.0 238.6 jit_solution(2747192408776111508)
XLA Ops:
  7.2 0.0 copy-start
  7.2 0.0 copy-start.3
  7.2 0.0 reduce-scatter.3.cloned.1.call-start
  7.2 1.8 copy-done
  9.1 4.0 %convert_add_fusion = f32[3072,512]{1,0:T(8,128)S(1)} fusion(bf16[512,3072]{1,0:T(8,128)(2,1)S(1)} %copy-done, bf16[512,512]{1,0:T(8,128)(2,1)} %param.5, bf16[1,3072,512]{2,1,0:T(8,128)(2,1)} %param.6), kind=kOutput, calls=%fused_computation | convolution fusion | flops 1613758464 | bytes 13107200 | tf_op jit(solution)/shard_map/dot_general | solution.py:21
  13.0 0.0 copy-start.1
  13.1 2.7 %copy-done.1 = f32[3072,512]{1,0:T(8,128)} copy-done((f32[3072,512]{1,0:T(8,128)}, f32[3072,512]{1,0:T(8,128)S(1)}, u32[]{:S(2)}) %copy-start.1) | copy-done | bytes 6291480
  15.7 0.0 copy-done.3
  15.7 7.1 %fusion.5 = f32[3072,64]{0,1:T(8,128)} fusion(f32[3072,512]{1,0:T(8,128)S(1)} %convert_add_fusion, f32[512,64]{0,1:T(8,128)S(1)} %copy-done.3), kind=kOutput, calls=%fused_computation.14 | convolution fusion | flops 1207959552 | bytes 7208960 | tf_op jit(solution)/shard_map/dot_general | solution.py:27
  22.8 0.0 reduce-scatter.3.cloned.1.call-update
  22.8 0.0 all-reduce.2.cloned.1.call-start
  22.9 37.8 %reduce-scatter.3.cloned.1.call-done = f32[384,64]{0,1:T(8,128)} async-done(((f32[3072,64]{0,1:T(8,128)}), f32[384,64]{0,1:T(8,128)}) %reduce-scatter.3.cloned.1.call-update) | async-done | bytes 98320 | tf_op jit(solution)/shard_map/reduce_scatter | solution.py:26
  60.6 0.0 all-reduce.2.cloned.1.call-update
  60.7 0.0 reduce-scatter.5.cloned.1.call-start
  60.7 36.7 %all-reduce.2.cloned.1.call-done = f32[384,64]{0,1:T(8,128)} async-done(((f32[384,64]{0,1:T(8,128)}), f32[384,64]{0,1:T(8,128)}) %all-reduce.2.cloned.1.call-update) | async-done | bytes 98320 | tf_op jit(solution)/shard_map/psum | solution.py:29
  97.4 1.2 fusion.6
  98.7 22.4 %psum.22 = f32[64,64]{0,1:T(8,128)S(1)} all-reduce(f32[64,64]{0,1:T(8,128)S(1)} %fusion.6), channel_id=1, replica_groups=mesh['cuts'=4,'dev'=8] {'dev'}, use_global_device_ids=true, to_apply=%region_2.0 | all-reduce | flops 4096 | bytes 32768 | tf_op jit(solution)/shard_map/psum | solution.py:30
  121.0 0.1 copy.8
  121.1 5.8 %cholesky.16 = f32[64,64]{1,0:T(8,128)S(1)} custom-call(f32[64,64]{1,0:T(8,128)S(1)} %fusion.4), custom_call_target="Cholesky" | custom-call | tf_op jit(solution)/shard_map/jit(cholesky)/cholesky | solution.py:10
  127.0 0.6 compare_reduce_fusion
  127.6 0.7 fusion.1
  128.3 4.9 %custom-call.6 = f32[1,64,64]{1,2,0:T(8,128)S(1)} custom-call(f32[1,64,64]{2,1,0:T(8,128)S(1)} %fusion.1), custom_call_target="InvertDiagBlocksLowerTriangular" | custom-call | tf_op jit(solution)/shard_map/triangular_solve | solution.py:11
  133.2 1.2 fusion.2
  134.4 11.1 %all_gather.6 = f32[3072,64]{0,1:T(8,128)S(1)} all-gather(f32[384,64]{0,1:T(8,128)S(1)} %fusion.2), channel_id=1, replica_groups=mesh['cuts'=4,'dev'=8] {'dev'}, dimensions={0}, use_global_device_ids=true | all-gather | bytes 884736 | tf_op jit(solution)/shard_map/all_gather | solution.py:32
  145.5 0.0 copy-start.2
  145.5 0.9 copy-done.2
  146.4 12.7 %fusion.7 = f32[512,64]{1,0:T(8,128)} fusion(f32[3072,512]{1,0:T(8,128)} %copy-done.1, f32[3072,64]{0,1:T(8,128)S(1)} %all_gather.6), kind=kOutput, calls=%fused_computation.16 | convolution fusion | flops 1207959552 | bytes 7208960 | tf_op jit(solution)/shard_map/dot_general | solution.py:15
  159.1 0.0 reduce-scatter.5.cloned.1.call-update
  159.1 32.7 %reduce-scatter.5.cloned.1.call-done = f32[64,64]{1,0:T(8,128)} async-done(((f32[512,64]{1,0:T(8,128)}), f32[64,64]{1,0:T(8,128)}) %reduce-scatter.5.cloned.1.call-update) | async-done | bytes 16400 | tf_op jit(solution)/shard_map/reduce_scatter | solution.py:33
  191.8 19.6 %psum.23 = f32[64,64]{1,0:T(8,128)S(1)} all-reduce(f32[64,64]{1,0:T(8,128)} %reduce-scatter.5.cloned.1.call-done), channel_id=1, replica_groups=mesh['cuts'=4,'dev'=8] {'cuts'}, use_global_device_ids=true, to_apply=%region_6.7 | all-reduce | flops 4096 | bytes 32768 | tf_op jit(solution)/shard_map/psum | solution.py:34
  211.4 9.2 %all_gather.7 = f32[512,64]{1,0:T(8,128)S(1)} all-gather(f32[64,64]{1,0:T(8,128)S(1)} %psum.23), channel_id=1, replica_groups=mesh['cuts'=4,'dev'=8] {'dev'}, dimensions={0}, use_global_device_ids=true | all-gather | bytes 147456 | tf_op jit(solution)/shard_map/all_gather | solution.py:35
  220.6 8.6 %fusion = bf16[1,3072,512]{2,1,0:T(8,128)(2,1)} fusion(f32[3072,512]{1,0:T(8,128)} %copy-done.1, f32[3072,64]{0,1:T(8,128)} %copy-done.2, f32[512,64]{1,0:T(8,128)S(1)} %all_gather.7), kind=kOutput, calls=%fused_computation.2 | convolution fusion | flops 1211138048 | bytes 10354688 | tf_op jit(solution)/shard_map/dot_general | solution.py:37
  229.2 0.8 copy.9
  230.0 2.1 copy.13
  (3 shorter events, 0.1 us)
Async XLA Ops:
  7.2 1.9 copy-start
  7.2 8.5 %copy-start.3 = (f32[512,64]{0,1:T(8,128)S(1)}, f32[512,64]{0,1:T(8,128)}, u32[]{:S(2)}) copy-start(f32[512,64]{0,1:T(8,128)} %param.7) | copy-start | bytes 393220
  7.2 53.5 %reduce-scatter.3.cloned.1.call-start = ((), (), s32[]{:S(2)}) async-start(), calls=%async_computation.2 | async-start | bytes 884736 | tf_op jit(solution)/shard_map/reduce_scatter | solution.py:26
  13.0 2.7 %copy-start.1 = (f32[3072,512]{1,0:T(8,128)}, f32[3072,512]{1,0:T(8,128)S(1)}, u32[]{:S(2)}) copy-start(f32[3072,512]{1,0:T(8,128)S(1)} %convert_add_fusion) | copy-start | bytes 18874372
  22.8 74.6 %all-reduce.2.cloned.1.call-start = ((), (), s32[]{:S(2)}) async-start(), calls=%async_computation.3 | async-start | bytes 196608 | tf_op jit(solution)/shard_map/psum | solution.py:29
  60.7 131.1 %reduce-scatter.5.cloned.1.call-start = ((), (), s32[]{:S(2)}) async-start(), calls=%async_computation.4 | async-start | bytes 294912 | tf_op jit(solution)/shard_map/reduce_scatter | solution.py:33
  145.5 0.9 copy-start.2
Sparse Core Ops, SparseCore 0:
  22.9 37.6 reduce-scatter.2
  63.0 34.4 all-reduce.1
  159.2 32.5 reduce-scatter.4
where the time goes:
time: 239 us
  waiting for transfers between devices  107 us (45%)
  blocking collectives  62.3 us (26%)
  matrix products  34.7 us (15%)
  between operations  13.8 us (6%)
  other arithmetic  12.1 us (5%)
  local copies, waits for them, and re-layouts  8.29 us (3%)
    reduce_scatter x1, waiting for transfers between devices, body(): lax.psum_scatter(jnp.dot(merged, previous_q, precision=HI), 'dev', scatte...  37.8 us
    psum x1, waiting for transfers between devices, body(): p_share = lax.psum(p_share, 'cuts')  36.7 us
    reduce_scatter x1, waiting for transfers between devices, body(): lax.psum_scatter(contract_rows(merged, p_hat), 'dev', scatter_dimension=0...  32.7 us
    psum x1, blocking collectives, body(): gram = lax.psum(contract_rows(p_share, p_share), 'dev')  22.4 us
    psum x1, blocking collectives, body(): q_share = lax.psum(q_share, 'cuts')  19.6 us
    dot_general x2, matrix products, contract_rows(): lax.dot_general(left, right, (((0,), (0,)), ((), ())), precision=HI, pref...  13.9 us
    all_gather x1, blocking collectives, body(): p_hat = lax.all_gather(hat_share, 'dev', axis=0, tiled=True)  11.1 us
    all_gather x1, blocking collectives, body(): q_sum = lax.all_gather(q_share, 'dev', axis=0, tiled=True)  9.24 us
  transfers between devices with their start and end apart: 3, of which 3 were waited for; matrix products, arithmetic and copies ran while one was open for 0% of the time, Pallas kernels for 0%

commit v1 on v0

--- a/solution.py
+++ b/solution.py
@@ -26,7 +26,11 @@
     p_share = lax.psum_scatter(
         jnp.dot(merged, previous_q, precision=HI), "dev", scatter_dimension=0, tiled=True
     )
-    p_share = lax.psum(p_share, "cuts")
+    count, acc = (lax.axis_size("cuts"), p_share)
+    for far in [1 << k for k in range(count.bit_length() - 1)]:
+        pairs = [(i, i ^ far) for i in range(count)]
+        acc = acc + lax.ppermute(acc, "cuts", pairs)
+    p_share = acc
     gram = lax.psum(contract_rows(p_share, p_share), "dev")
     hat_share = solve_factor(gram, p_share)
     p_hat = lax.all_gather(hat_share, "dev", axis=0, tiled=True)

time: 239 us -> 214 us (0.90)
  waiting for transfers between devices: 107 us -> 79.1 us
  starting transfers between devices: 0.12 us -> 4.04 us
    psum x1 -> x0, waiting for transfers between devices: 36.7 us -> none  [body(): p_share = lax.psum(p_share, 'cuts')]
    ppermute x0 -> x2, waiting for transfers between devices: none -> 7.5 us  [body(): acc = acc + lax.ppermute(acc, 'cuts', pairs)]
    ppermute x0 -> x2, starting transfers between devices: none -> 3.96 us  [body(): acc = acc + lax.ppermute(acc, 'cuts', pairs)]
  transfers between devices with their start and end apart: 3 -> 4, of which waited for: 3 -> 4; matrix products, arithmetic and copies ran while one was open for 0% -> 0% of each run, Pallas kernels for 0% -> 0%
where the time goes in v1:
time: 214 us
  waiting for transfers between devices  79.1 us (37%)
  blocking collectives  62.3 us (29%)
  matrix products  32.9 us (15%)
  between operations  14.1 us (7%)
  other arithmetic  13 us (6%)
  local copies, waits for them, and re-layouts  8.29 us (4%)
  starting transfers between devices  4.04 us (2%)
    reduce_scatter x1, waiting for transfers between devices, body(): lax.psum_scatter(jnp.dot(merged, previous_q, precision=HI), 'dev', scatte...  37.8 us
    reduce_scatter x1, waiting for transfers between devices, body(): lax.psum_scatter(contract_rows(merged, p_hat), 'dev', scatter_dimension=0...  33.8 us
    psum x1, blocking collectives, body(): gram = lax.psum(contract_rows(p_share, p_share), 'dev')  22.4 us
    psum x1, blocking collectives, body(): q_share = lax.psum(q_share, 'cuts')  19.6 us
    dot_general x2, matrix products, contract_rows(): lax.dot_general(left, right, (((0,), (0,)), ((), ())), precision=HI, pref...  13 us
    all_gather x1, blocking collectives, body(): p_hat = lax.all_gather(hat_share, 'dev', axis=0, tiled=True)  11.1 us
    all_gather x1, blocking collectives, body(): q_sum = lax.all_gather(q_share, 'dev', axis=0, tiled=True)  9.25 us
    dot_general x1, matrix products, body(): approx = jnp.dot(p_hat, q_mean.T, precision=HI)  8.56 us
  transfers between devices with their start and end apart: 4, of which 4 were waited for; matrix products, arithmetic and copies ran while one was open for 0% of the time, Pallas kernels for 0%

profile of v1, /device:TPU:0, one launch (start us, length us, event | category | flops | bytes accessed | tf_op | source)
XLA Modules:
  0.0 213.8 jit_solution(2686181883835082658)
XLA Ops:
  7.2 0.0 copy-start
  7.2 0.0 copy-start.3
  7.2 0.0 reduce-scatter.3.cloned.1.call-start
  7.2 1.8 copy-done
  9.1 4.0 %convert_add_fusion = f32[3072,512]{1,0:T(8,128)S(1)} fusion(bf16[512,3072]{1,0:T(8,128)(2,1)S(1)} %copy-done, bf16[512,512]{1,0:T(8,128)(2,1)} %param.5, bf16[1,3072,512]{2,1,0:T(8,128)(2,1)} %param.6), kind=kOutput, calls=%fused_computation | convolution fusion | flops 1613758464 | bytes 13107200 | tf_op jit(solution)/shard_map/dot_general | solution.py:21
  13.0 0.0 copy-start.1
  13.1 2.7 %copy-done.1 = f32[3072,512]{1,0:T(8,128)} copy-done((f32[3072,512]{1,0:T(8,128)}, f32[3072,512]{1,0:T(8,128)S(1)}, u32[]{:S(2)}) %copy-start.1) | copy-done | bytes 6291480
  15.7 0.0 copy-done.3
  15.7 7.1 %fusion.5 = f32[3072,64]{0,1:T(8,128)} fusion(f32[3072,512]{1,0:T(8,128)S(1)} %convert_add_fusion, f32[512,64]{0,1:T(8,128)S(1)} %copy-done.3), kind=kOutput, calls=%fused_computation.14 | convolution fusion | flops 1207959552 | bytes 7208960 | tf_op jit(solution)/shard_map/dot_general | solution.py:27
  22.8 0.0 reduce-scatter.3.cloned.1.call-update
  22.8 0.0 reduce-scatter.5.cloned.1.call-start
  22.9 37.8 %reduce-scatter.3.cloned.1.call-done = f32[384,64]{0,1:T(8,128)} async-done(((f32[3072,64]{0,1:T(8,128)}), f32[384,64]{0,1:T(8,128)}) %reduce-scatter.3.cloned.1.call-update) | async-done | bytes 98320 | tf_op jit(solution)/shard_map/reduce_scatter | solution.py:26
  60.6 1.5 collective-permute-start
  62.1 3.3 %collective-permute-done = f32[384,64]{0,1:T(8,128)S(1)} collective-permute-done((f32[384,64]{0,1:T(8,128)}, f32[384,64]{0,1:T(8,128)S(1)}, u32[]{:S(2)}, u32[]{:S(2)}) %collective-permute-start) | collective-permute-done | bytes 98336 | tf_op jit(solution)/shard_map/ppermute | solution.py:32
  65.5 0.9 add.29
  66.4 2.5 %collective-permute-start.1 = (f32[384,64]{0,1:T(8,128)S(1)}, f32[384,64]{0,1:T(8,128)S(1)}, u32[]{:S(2)}, u32[]{:S(2)}) collective-permute-start(f32[384,64]{0,1:T(8,128)S(1)} %add.29), channel_id=1, source_target_pairs={{0,16},{8,24},{16,0},{24,8},{1,17},{9,25},{17,1},{25,9},{2,18},{10... | collective-permute-start | bytes 294920 | tf_op jit(solution)/shard_map/ppermute | solution.py:32
  68.9 4.2 %collective-permute-done.1 = f32[384,64]{0,1:T(8,128)S(1)} collective-permute-done((f32[384,64]{0,1:T(8,128)S(1)}, f32[384,64]{0,1:T(8,128)S(1)}, u32[]{:S(2)}, u32[]{:S(2)}) %collective-permute-start.1) | collective-permute-done | bytes 98336 | tf_op jit(solution)/shard_map/ppermute | solution.py:32
  73.0 0.3 fusion.6
  73.3 22.4 %psum.14 = f32[64,64]{0,1:T(8,128)S(1)} all-reduce(f32[64,64]{0,1:T(8,128)S(1)} %fusion.6), channel_id=1, replica_groups=mesh['cuts'=4,'dev'=8] {'dev'}, use_global_device_ids=true, to_apply=%region_1.0 | all-reduce | flops 4096 | bytes 32768 | tf_op jit(solution)/shard_map/psum | solution.py:34
  95.6 0.1 copy.8
  95.7 5.8 %cholesky.16 = f32[64,64]{1,0:T(8,128)S(1)} custom-call(f32[64,64]{1,0:T(8,128)S(1)} %fusion.4), custom_call_target="Cholesky" | custom-call | tf_op jit(solution)/shard_map/jit(cholesky)/cholesky | solution.py:10
  101.6 0.6 compare_reduce_fusion
  102.3 0.7 fusion.1
  102.9 4.9 %custom-call.6 = f32[1,64,64]{1,2,0:T(8,128)S(1)} custom-call(f32[1,64,64]{2,1,0:T(8,128)S(1)} %fusion.1), custom_call_target="InvertDiagBlocksLowerTriangular" | custom-call | tf_op jit(solution)/shard_map/triangular_solve | solution.py:11
  107.8 0.3 fusion.2
  108.1 11.1 %all_gather.6 = f32[3072,64]{0,1:T(8,128)S(1)} all-gather(f32[384,64]{0,1:T(8,128)S(1)} %fusion.2), channel_id=1, replica_groups=mesh['cuts'=4,'dev'=8] {'dev'}, dimensions={0}, use_global_device_ids=true | all-gather | bytes 884736 | tf_op jit(solution)/shard_map/all_gather | solution.py:36
  119.2 0.0 copy-start.2
  119.2 0.9 copy-done.2
  120.1 12.7 %fusion.7 = f32[512,64]{1,0:T(8,128)} fusion(f32[3072,512]{1,0:T(8,128)} %copy-done.1, f32[3072,64]{0,1:T(8,128)S(1)} %all_gather.6), kind=kOutput, calls=%fused_computation.16 | convolution fusion | flops 1207959552 | bytes 7208960 | tf_op jit(solution)/shard_map/dot_general | solution.py:15
  132.8 0.0 reduce-scatter.5.cloned.1.call-update
  132.8 33.8 %reduce-scatter.5.cloned.1.call-done = f32[64,64]{1,0:T(8,128)} async-done(((f32[512,64]{1,0:T(8,128)}), f32[64,64]{1,0:T(8,128)}) %reduce-scatter.5.cloned.1.call-update) | async-done | bytes 16400 | tf_op jit(solution)/shard_map/reduce_scatter | solution.py:37
  166.6 19.6 %psum.15 = f32[64,64]{1,0:T(8,128)S(1)} all-reduce(f32[64,64]{1,0:T(8,128)} %reduce-scatter.5.cloned.1.call-done), channel_id=1, replica_groups=mesh['cuts'=4,'dev'=8] {'cuts'}, use_global_device_ids=true, to_apply=%region_5.6 | all-reduce | flops 4096 | bytes 32768 | tf_op jit(solution)/shard_map/psum | solution.py:38
  186.2 9.2 %all_gather.7 = f32[512,64]{1,0:T(8,128)S(1)} all-gather(f32[64,64]{1,0:T(8,128)S(1)} %psum.15), channel_id=1, replica_groups=mesh['cuts'=4,'dev'=8] {'dev'}, dimensions={0}, use_global_device_ids=true | all-gather | bytes 147456 | tf_op jit(solution)/shard_map/all_gather | solution.py:39
  195.5 8.6 %fusion = bf16[1,3072,512]{2,1,0:T(8,128)(2,1)} fusion(f32[3072,512]{1,0:T(8,128)} %copy-done.1, f32[3072,64]{0,1:T(8,128)} %copy-done.2, f32[512,64]{1,0:T(8,128)S(1)} %all_gather.7), kind=kOutput, calls=%fused_computation.2 | convolution fusion | flops 1211138048 | bytes 10354688 | tf_op jit(solution)/shard_map/dot_general | solution.py:41
  204.1 0.8 copy.9
  204.8 2.1 copy.12
  (4 shorter events, 0.1 us)
Async XLA Ops:
  7.2 1.9 copy-start
  7.2 8.5 %copy-start.3 = (f32[512,64]{0,1:T(8,128)S(1)}, f32[512,64]{0,1:T(8,128)}, u32[]{:S(2)}) copy-start(f32[512,64]{0,1:T(8,128)} %param.7) | copy-start | bytes 393220
  7.2 53.5 %reduce-scatter.3.cloned.1.call-start = ((), (), s32[]{:S(2)}) async-start(), calls=%async_computation.2 | async-start | bytes 884736 | tf_op jit(solution)/shard_map/reduce_scatter | solution.py:26
  13.0 2.7 %copy-start.1 = (f32[3072,512]{1,0:T(8,128)}, f32[3072,512]{1,0:T(8,128)S(1)}, u32[]{:S(2)}) copy-start(f32[3072,512]{1,0:T(8,128)S(1)} %convert_add_fusion) | copy-start | bytes 18874372
  22.8 143.8 %reduce-scatter.5.cloned.1.call-start = ((), (), s32[]{:S(2)}) async-start(), calls=%async_computation.3 | async-start | bytes 294912 | tf_op jit(solution)/shard_map/reduce_scatter | solution.py:37
  60.6 4.8 %collective-permute-start = (f32[384,64]{0,1:T(8,128)}, f32[384,64]{0,1:T(8,128)S(1)}, u32[]{:S(2)}, u32[]{:S(2)}) collective-permute-start(f32[384,64]{0,1:T(8,128)} %reduce-scatter.3.cloned.1.call-done), channel_id=1, source_target_pairs={{0,8},{8,0},{16,24},{24,16},{1,9},{9,1},{17,25},{25,17},{2,10},{10... | collective-permute-start | bytes 294920 | tf_op jit(solution)/shard_map/ppermute | solution.py:32
  66.4 6.6 %collective-permute-start.1 = (f32[384,64]{0,1:T(8,128)S(1)}, f32[384,64]{0,1:T(8,128)S(1)}, u32[]{:S(2)}, u32[]{:S(2)}) collective-permute-start(f32[384,64]{0,1:T(8,128)S(1)} %add.29), channel_id=1, source_target_pairs={{0,16},{8,24},{16,0},{24,8},{1,17},{9,25},{17,1},{25,9},{2,18},{10... | collective-permute-start | bytes 294920 | tf_op jit(solution)/shard_map/ppermute | solution.py:32
  119.2 0.9 copy-start.2
Sparse Core Ops, SparseCore 0:
  22.9 37.6 reduce-scatter.2
  132.9 33.6 reduce-scatter.4
